TPU v7x, 512 devices: a whole 4x8x8 slice. The times are simulated.
512 devices in a mesh: section: 8 (over y_lo, core), dp: 64 (over y_hi, x, z).
Axes of the slice: x: 4, y: 8 (y_hi: 2, y_lo: 4; y = y_hi * 4 + y_lo), z: 8, core: 2. Of those that a mesh axis runs over, the one named last changes fastest.
Arguments:
- tokens: int32 [8, 5120], P(None, 'dp'), may hold values from 0 to 255
- doc_patches: int32 [8], replicated, may hold values from 160 to 640, as said below
- global_embed: bfloat16 [8, 640, 4096], P('section', 'dp'), may hold values from -6 to 6
- byte_table: bfloat16 [256, 1024], replicated, may hold values from -6 to 6
- w_qkv: bfloat16 [8, 1024, 3072], P('section', 'dp'), may hold values from -0.1875 to 0.1875
- w_out: bfloat16 [8, 1024, 1024], P('section', 'dp'), may hold values from -0.1875 to 0.1875
- layer_gain: bfloat16 [8, 1024], P('section'), may hold values from 0.099609375 to 1.8984375
- w_global: bfloat16 [512, 1024], P(None, 'dp'), may hold values from -0.25 to 0.25
- final_gain: bfloat16 [1024], replicated, may hold values from 0.099609375 to 1.8984375
- w_head: bfloat16 [256, 1024], P(None, 'dp'), may hold values from -0.59765625 to 0.59765625
Outputs:
- logits: bfloat16 [8, 5120, 256], P('section', 'dp')
Inputs may be any that keep to these rules, and one draw needn't show every extreme that they name: Patches from index doc_patches[m] on are padding of micro-batch m; the micro-batches' counts differ from one another.
All inputs are finite; a program needn't handle non-finite values.
Results may differ from a plain program's by a relative error of at most 0.014.
Values may be sent and summed in bfloat16 or wider, within the bound.
No kernel may reach another device: no remote copies, remote signals or barrier semaphores. Data moves between devices by JAX's collectives and lax.ppermute only.
A program may use at most 64 MiB of HBM per device.

v0:
```python
import jax
import jax.numpy as jnp
from jax import lax
from jax.sharding import PartitionSpec as P

HEADS = 16
PATCH = 8


def gather_turned(arrays, axis, dims):
    turned = [jnp.moveaxis(a, dim, 0) for a, dim in zip(arrays, dims)]
    both = jnp.concatenate([t.reshape(len(t), -1) for t in turned], axis=1)
    filled, at, gathered = (lax.all_gather(both, axis, axis=0, tiled=True), 0, [])
    for t, dim in zip(turned, dims):
        piece = filled[:, at : at + t[0].size].reshape(-1, *t.shape[1:])
        gathered.append(jnp.moveaxis(piece, 0, dim))
        at += t[0].size
    return tuple(gathered)


def copy_for_each(shard, axis):
    copies = jnp.broadcast_to(shard, (lax.axis_size(axis), *shard.shape))
    return lax.all_to_all(copies, axis, split_axis=0, concat_axis=0, tiled=True)


def joined_along(pieces, dim):
    lengths = list(pieces.shape[1:])
    lengths[dim] *= pieces.shape[0]
    return jnp.moveaxis(pieces, 0, dim).reshape(lengths)


def gathered_copies(shard, axis, dim):
    pieces = copy_for_each(shard, axis)
    return joined_along(pieces, dim)


def from_behind(block, axis, distance):
    devices = range(lax.axis_size(axis))
    route = [(i - distance, i) for i in devices if i - distance in devices]
    return lax.ppermute(block, axis, route)


def broadcast(shard, axis, root):
    return lax.dynamic_index_in_dim(lax.all_gather(shard, axis), root, 0, keepdims=False)


def norm_rows(hidden, norm_gain):
    scale = lax.rsqrt(jnp.mean(hidden * hidden, axis=-1, keepdims=True) + 1e-06)
    return (hidden * scale * norm_gain.astype(jnp.float32)).astype(jnp.bfloat16)


def attend_layer(inputs, global_add, norm_gain, qkv_weight, out_weight):
    hidden = inputs.astype(jnp.float32) + global_add.astype(jnp.float32)
    normed = norm_rows(hidden, norm_gain)
    projected = jnp.dot(normed, qkv_weight, preferred_element_type=jnp.float32).astype(jnp.bfloat16)
    model_width = inputs.shape[1]
    head_dim = model_width // HEADS
    patch_count = inputs.shape[0] // PATCH

    def split_heads(block):
        return block.reshape(patch_count, PATCH, HEADS, head_dim)

    queries = split_heads(projected[:, :model_width])
    key_rows = split_heads(projected[:, model_width : 2 * model_width])
    value_rows = split_heads(projected[:, 2 * model_width :])
    scores = jnp.einsum(
        "pqhd,pkhd->phqk", queries, key_rows, preferred_element_type=jnp.float32
    ) * head_dim ** (-0.5)
    causal = jnp.tril(jnp.ones((PATCH, PATCH), dtype=jnp.bool_))
    scores = jnp.where(causal, scores, -1e30)
    weights = jax.nn.softmax(scores, axis=-1).astype(jnp.bfloat16)
    context = jnp.einsum("phqk,pkhd->pqhd", weights, value_rows, preferred_element_type=jnp.float32)
    context = context.astype(jnp.bfloat16).reshape(inputs.shape[0], model_width)
    return (hidden + jnp.dot(context, out_weight, preferred_element_type=jnp.float32)).astype(
        jnp.bfloat16
    )


def previous_bytes(byte_ids):
    blocks = byte_ids.reshape(-1, PATCH)
    shifted = jnp.concatenate([jnp.zeros((blocks.shape[0], 1), jnp.int32), blocks[:, :-1]], axis=1)
    return shifted.reshape(-1)


def shards(
    tokens,
    doc_patches,
    global_embed,
    byte_table,
    w_qkv,
    w_out,
    layer_gain,
    w_global,
    final_gain,
    w_head,
):
    sections = lax.axis_size("section")
    section_index = lax.axis_index("section")
    column_index = lax.axis_index("dp")
    micro_count, row_count = tokens.shape
    held_micro = global_embed.shape[0]
    model_width = byte_table.shape[1]
    qkv_full, out_full, global_full, head_full = gather_turned(
        (w_qkv, w_out, w_global, w_head), "dp", (1, 1, 1, 1)
    )
    qkv_full = qkv_full[0]
    out_full = out_full[0]
    norm_gain = layer_gain[0]
    byte_ids = previous_bytes(tokens.reshape(-1))
    one_hot = (
        byte_ids[:, None] == jnp.arange(byte_table.shape[0], dtype=jnp.int32)[None, :]
    ).astype(jnp.bfloat16)
    embeds = jnp.dot(one_hot, byte_table, preferred_element_type=jnp.float32).astype(jnp.bfloat16)
    embeds = embeds.reshape(micro_count, row_count, model_width)
    gathered = gathered_copies(global_embed, "section", 0)
    global_add = jnp.dot(
        gathered.reshape(micro_count * row_count, -1),
        global_full,
        preferred_element_type=jnp.float32,
    )
    global_add = global_add.astype(jnp.bfloat16).reshape(micro_count, row_count, model_width)

    def advance(moment, state):
        incoming, finals = state
        micro_index = moment - section_index
        active = (micro_index >= 0) & (micro_index < micro_count)
        picked = jnp.clip(micro_index, 0, micro_count - 1)
        fresh = lax.dynamic_index_in_dim(embeds, picked, 0, keepdims=False)
        inputs = jnp.where(section_index == 0, fresh, incoming)
        added = lax.dynamic_index_in_dim(global_add, picked, 0, keepdims=False)
        result = lax.cond(
            active,
            lambda: attend_layer(inputs, added, norm_gain, qkv_full, out_full),
            lambda: jnp.zeros_like(inputs),
        )
        previous = lax.dynamic_index_in_dim(finals, picked, 0, keepdims=False)
        keeping = active & (section_index == sections - 1)
        finals = lax.dynamic_update_index_in_dim(
            finals, jnp.where(keeping, result, previous), picked, 0
        )
        incoming = from_behind(result, "section", 1)
        return (incoming, finals)

    initial = (
        jnp.zeros((row_count, model_width), jnp.bfloat16),
        jnp.zeros((micro_count, row_count, model_width), jnp.bfloat16),
    )
    incoming, finals = lax.fori_loop(0, micro_count + sections - 1, advance, initial)
    final_rows = norm_rows(finals.reshape(-1, model_width).astype(jnp.float32), final_gain)
    scores = jnp.einsum("rd,vd->rv", final_rows, head_full, preferred_element_type=jnp.float32)
    scores = scores.reshape(micro_count, row_count, -1)
    patch_start = column_index * (row_count // PATCH)
    patch_of_row = patch_start + jnp.arange(row_count, dtype=jnp.int32) // PATCH
    live_rows = patch_of_row[None, :] < doc_patches[:, None]
    masked = jnp.where(live_rows[:, :, None], scores, 0.0).astype(jnp.bfloat16)
    everyone = broadcast(masked, "section", sections - 1)
    return lax.dynamic_slice_in_dim(everyone, section_index * held_micro, held_micro, 0)


def solution(mesh):
    in_specs = (
        P(None, "dp"),
        P(),
        P("section", "dp", None),
        P(),
        P("section", "dp", None),
        P("section", "dp", None),
        P("section", None),
        P(None, "dp"),
        P(),
        P(None, "dp"),
    )
    out_specs = P("section", "dp", None)
    return jax.shard_map(shards, mesh=mesh, in_specs=in_specs, out_specs=out_specs, check_vma=False)
```

profile of v0, /device:TPU:57, one launch (start us, length us, event | category | flops | bytes accessed | tf_op | source)
XLA Modules:
  0.0 610.4 jit_solution(12505963879059511700)
XLA Ops:
  6.6 1.7 pad_maximum_fusion
  8.3 2.0 broadcast_in_dim.54
  10.3 6.7 %all-to-all-start = ((bf16[8,1,10,4096]{3,2,1,0:T(8,128)(2,1)}), bf16[8,1,10,4096]{3,2,1,0:T(8,128)(2,1)S(1)}, u32[]{:S(2)}, u32[]{:S(2)}) async-start(bf16[8,1,10,4096]{3,2,1,0:T(8,128)(2,1)} %broadcast_in_dim.54), calls=%async_computation | async-start | bytes 2097152 | tf_op jit(solution)/shard_map/all_to_all | solution.py:23
  19.0 24.2 %all-to-all-done = bf16[8,1,10,4096]{3,2,1,0:T(8,128)(2,1)S(1)} async-done(((bf16[8,1,10,4096]{3,2,1,0:T(8,128)(2,1)}), bf16[8,1,10,4096]{3,2,1,0:T(8,128)(2,1)S(1)}, u32[]{:S(2)}, u32[]{:S(2)}) %all-to-all-start) | async-done | bytes 655392 | tf_op jit(solution)/shard_map/all_to_all | solution.py:23
  43.7 165.9 %all-gather.4.cloned.1.call-done = bf16[1024,4864]{1,0:T(8,128)(2,1)} async-done(((bf16[16,4864]{1,0:T(8,128)(2,1)}), bf16[1024,4864]{1,0:T(8,128)(2,1)}) %all-gather.4.cloned.1.call-update) | async-done | bytes 9961488 | tf_op jit(solution)/shard_map/all_gather | solution.py:13
  209.6 5.9 slice.42
  215.5 1.8 slice.43
  217.3 3.2 convolution_convert_fusion.2
  221.7 325.8 %while.16 = (s32[]{:T(128)}, bf16[80,1024]{1,0:T(8,128)(2,1)S(1)}, bf16[8,80,1024]{2,1,0:T(8,128)(2,1)}, s32[]{:T(128)}, pred[]{:T(512)}, /*index=5*/bf16[8,80,1...) while((s32[]{:T(128)}, bf16[80,1024]{1,0:T(8,128)(2,1)S(1)}, ...), condition=%wide.region_6.7_spmd, body=%wide.region_0.6_spmd.sunk | while | flops 676917632 | bytes 15702796 | solution.py:148
  225.4 2.0 collective-permute-done
  231.0 10.1 %collective-permute-done = bf16[80,1024]{1,0:T(8,128)(2,1)S(1)} collective-permute-done((bf16[80,1024]{1,0:T(8,128)(2,1)}, bf16[80,1024]{1,0:T(8,128)(2,1)S(1)}, u32[]{:S(2)}, u32[]{:S(2)}) %collective-permute-start) | collective-permute-done | bytes 163872 | tf_op jit(solution)/shard_map/while/body/eval_jaxpr/ppermute | solution.py:40
  244.7 3.9 collective-permute-done
  252.3 3.9 collective-permute-done
  259.8 3.9 collective-permute-done
  267.3 3.9 collective-permute-done
  274.8 89.9 %collective-permute-done = bf16[80,1024]{1,0:T(8,128)(2,1)S(1)} collective-permute-done((bf16[80,1024]{1,0:T(8,128)(2,1)}, bf16[80,1024]{1,0:T(8,128)(2,1)S(1)}, u32[]{:S(2)}, u32[]{:S(2)}) %collective-permute-start) | collective-permute-done | bytes 163872 | tf_op jit(solution)/shard_map/while/body/eval_jaxpr/ppermute | solution.py:40
  364.7 16.4 %conditional.2 = (bf16[80,1024]{1,0:T(8,128)(2,1)}) conditional(s32[]{:T(128)} %convert_element_type.127, () %tuple.47, (pred[]{:T(512)}, bf16[8,80,1024]{2,1,0:T(8,128)(2,1)}, s32[]{:T(128)}, bf16[80,1024]{1,0:T(8,128)(2,1)S(1)}, bf16[8,80,1024]{2,1,0:T(8,128)(2,1)}, /*index=5*/bf16[1024]{0:T(1024)(128)(2,1)S(1)}, bf16[1024,3072]{1,0:T(8,128)(2,1)}, ...), branch_computations={%region_1.1_spmd, %region_2.5_spmd} | conditional | flops 676835712 | bytes 14227409 | solution.py:131
  365.9 4.2 convolution_convert_fusion
  375.2 2.5 fusion.4
  379.0 2.1 fusion.5
  383.3 1.6 bitcast_dynamic-update-slice_fusion.2
  385.0 3.0 collective-permute-done
  387.9 16.4 %conditional.2 = (bf16[80,1024]{1,0:T(8,128)(2,1)}) conditional(s32[]{:T(128)} %convert_element_type.127, () %tuple.47, (pred[]{:T(512)}, bf16[8,80,1024]{2,1,0:T(8,128)(2,1)}, s32[]{:T(128)}, bf16[80,1024]{1,0:T(8,128)(2,1)S(1)}, bf16[8,80,1024]{2,1,0:T(8,128)(2,1)}, /*index=5*/bf16[1024]{0:T(1024)(128)(2,1)S(1)}, bf16[1024,3072]{1,0:T(8,128)(2,1)}, ...), branch_computations={%region_1.1_spmd, %region_2.5_spmd} | conditional | flops 676835712 | bytes 14227409 | solution.py:131
  389.1 4.2 convolution_convert_fusion
  398.5 2.5 fusion.4
  402.2 2.1 fusion.5
  408.2 3.0 collective-permute-done
  411.1 16.4 %conditional.2 = (bf16[80,1024]{1,0:T(8,128)(2,1)}) conditional(s32[]{:T(128)} %convert_element_type.127, () %tuple.47, (pred[]{:T(512)}, bf16[8,80,1024]{2,1,0:T(8,128)(2,1)}, s32[]{:T(128)}, bf16[80,1024]{1,0:T(8,128)(2,1)S(1)}, bf16[8,80,1024]{2,1,0:T(8,128)(2,1)}, /*index=5*/bf16[1024]{0:T(1024)(128)(2,1)S(1)}, bf16[1024,3072]{1,0:T(8,128)(2,1)}, ...), branch_computations={%region_1.1_spmd, %region_2.5_spmd} | conditional | flops 676835712 | bytes 14227409 | solution.py:131
  412.3 4.2 convolution_convert_fusion
  421.7 2.5 fusion.4
  425.4 2.1 fusion.5
  429.8 1.6 bitcast_dynamic-update-slice_fusion.2
  431.4 3.0 collective-permute-done
  434.4 16.4 %conditional.2 = (bf16[80,1024]{1,0:T(8,128)(2,1)}) conditional(s32[]{:T(128)} %convert_element_type.127, () %tuple.47, (pred[]{:T(512)}, bf16[8,80,1024]{2,1,0:T(8,128)(2,1)}, s32[]{:T(128)}, bf16[80,1024]{1,0:T(8,128)(2,1)S(1)}, bf16[8,80,1024]{2,1,0:T(8,128)(2,1)}, /*index=5*/bf16[1024]{0:T(1024)(128)(2,1)S(1)}, bf16[1024,3072]{1,0:T(8,128)(2,1)}, ...), branch_computations={%region_1.1_spmd, %region_2.5_spmd} | conditional | flops 676835712 | bytes 14227409 | solution.py:131
  435.6 4.2 convolution_convert_fusion
  444.9 2.5 fusion.4
  448.7 2.1 fusion.5
  454.6 3.0 collective-permute-done
  457.6 16.4 %conditional.2 = (bf16[80,1024]{1,0:T(8,128)(2,1)}) conditional(s32[]{:T(128)} %convert_element_type.127, () %tuple.47, (pred[]{:T(512)}, bf16[8,80,1024]{2,1,0:T(8,128)(2,1)}, s32[]{:T(128)}, bf16[80,1024]{1,0:T(8,128)(2,1)S(1)}, bf16[8,80,1024]{2,1,0:T(8,128)(2,1)}, /*index=5*/bf16[1024]{0:T(1024)(128)(2,1)S(1)}, bf16[1024,3072]{1,0:T(8,128)(2,1)}, ...), branch_computations={%region_1.1_spmd, %region_2.5_spmd} | conditional | flops 676835712 | bytes 14227409 | solution.py:131
  458.8 4.2 convolution_convert_fusion
  468.1 2.5 fusion.4
  471.9 2.1 fusion.5
  476.2 1.6 bitcast_dynamic-update-slice_fusion.2
  477.8 3.0 collective-permute-done
  480.8 16.4 %conditional.2 = (bf16[80,1024]{1,0:T(8,128)(2,1)}) conditional(s32[]{:T(128)} %convert_element_type.127, () %tuple.47, (pred[]{:T(512)}, bf16[8,80,1024]{2,1,0:T(8,128)(2,1)}, s32[]{:T(128)}, bf16[80,1024]{1,0:T(8,128)(2,1)S(1)}, bf16[8,80,1024]{2,1,0:T(8,128)(2,1)}, /*index=5*/bf16[1024]{0:T(1024)(128)(2,1)S(1)}, bf16[1024,3072]{1,0:T(8,128)(2,1)}, ...), branch_computations={%region_1.1_spmd, %region_2.5_spmd} | conditional | flops 676835712 | bytes 14227409 | solution.py:131
  482.0 4.2 convolution_convert_fusion
  491.3 2.5 fusion.4
  495.1 2.1 fusion.5
  499.4 1.6 bitcast_dynamic-update-slice_fusion.2
  501.1 3.0 collective-permute-done
  504.0 16.4 %conditional.2 = (bf16[80,1024]{1,0:T(8,128)(2,1)}) conditional(s32[]{:T(128)} %convert_element_type.127, () %tuple.47, (pred[]{:T(512)}, bf16[8,80,1024]{2,1,0:T(8,128)(2,1)}, s32[]{:T(128)}, bf16[80,1024]{1,0:T(8,128)(2,1)S(1)}, bf16[8,80,1024]{2,1,0:T(8,128)(2,1)}, /*index=5*/bf16[1024]{0:T(1024)(128)(2,1)S(1)}, bf16[1024,3072]{1,0:T(8,128)(2,1)}, ...), branch_computations={%region_1.1_spmd, %region_2.5_spmd} | conditional | flops 676835712 | bytes 14227409 | solution.py:131
  505.2 4.2 convolution_convert_fusion
  514.5 2.5 fusion.4
  518.3 2.1 fusion.5
  522.6 1.6 bitcast_dynamic-update-slice_fusion.2
  524.3 3.0 collective-permute-done
  527.2 16.4 %conditional.2 = (bf16[80,1024]{1,0:T(8,128)(2,1)}) conditional(s32[]{:T(128)} %convert_element_type.127, () %tuple.47, (pred[]{:T(512)}, bf16[8,80,1024]{2,1,0:T(8,128)(2,1)}, s32[]{:T(128)}, bf16[80,1024]{1,0:T(8,128)(2,1)S(1)}, bf16[8,80,1024]{2,1,0:T(8,128)(2,1)}, /*index=5*/bf16[1024]{0:T(1024)(128)(2,1)S(1)}, bf16[1024,3072]{1,0:T(8,128)(2,1)}, ...), branch_computations={%region_1.1_spmd, %region_2.5_spmd} | conditional | flops 676835712 | bytes 14227409 | solution.py:131
  528.4 4.2 convolution_convert_fusion
  537.8 2.5 fusion.4
  541.5 2.1 fusion.5
  545.8 1.6 bitcast_dynamic-update-slice_fusion.2
  547.5 1.7 fusion.19
  549.2 2.7 fusion.29
  551.9 50.0 %all-gather.6.cloned.1.call-done = bf16[64,80,256]{2,1,0:T(8,128)(2,1)} async-done(((bf16[8,80,256]{2,1,0:T(8,128)(2,1)}), bf16[64,80,256]{2,1,0:T(8,128)(2,1)}) %all-gather.6.cloned.1.call-update) | async-done | bytes 2621456 | tf_op jit(solution)/shard_map/all_gather | solution.py:44
  (178 shorter events, 117.0 us)
Async XLA Ops:
  6.5 10.9 %copy-start = (bf16[256,1024]{1,0:T(8,128)(2,1)S(1)}, bf16[256,1024]{1,0:T(8,128)(2,1)}, u32[]{:S(2)}) copy-start(bf16[256,1024]{1,0:T(8,128)(2,1)} %param.17) | copy-start | bytes 1572868
  6.5 10.5 %copy-start.2 = (s32[8,80]{1,0:T(8,128)S(1)}, s32[8,80]{1,0:T(8,128)}, u32[]{:S(2)}) copy-start(s32[8,80]{1,0:T(8,128)} %param.14) | copy-start | bytes 7684
  6.5 10.8 %copy-start.3 = (bf16[1024]{0:T(1024)(128)(2,1)S(1)}, bf16[1024]{0:T(1024)(128)(2,1)}, u32[]{:S(2)}) copy-start(bf16[1024]{0:T(1024)(128)(2,1)} %param.22) | copy-start | bytes 6148
  6.5 10.8 %copy-start.1 = (bf16[1,1024]{1,0:T(2,128)(2,1)S(1)}, bf16[1,1024]{1,0:T(2,128)(2,1)}, u32[]{:S(2)}) copy-start(bf16[1,1024]{1,0:T(2,128)(2,1)} %param.20) | copy-start | bytes 6148
  6.5 10.8 %copy-start.4 = (s32[8]{0:T(128)S(1)}, s32[8]{0:T(128)}, u32[]{:S(2)}) copy-start(s32[8]{0:T(128)} %param.15) | copy-start | bytes 100
  6.5 203.1 %all-gather.4.cloned.1.call-start = ((), (), s32[]{:S(2)}) async-start(), calls=%async_computation.1 | async-start | bytes 10117120 | tf_op jit(solution)/shard_map/all_gather | solution.py:13
  10.3 32.9 %all-to-all-start = ((bf16[8,1,10,4096]{3,2,1,0:T(8,128)(2,1)}), bf16[8,1,10,4096]{3,2,1,0:T(8,128)(2,1)S(1)}, u32[]{:S(2)}, u32[]{:S(2)}) async-start(bf16[8,1,10,4096]{3,2,1,0:T(8,128)(2,1)} %broadcast_in_dim.54), calls=%async_computation | async-start | bytes 2097152 | tf_op jit(solution)/shard_map/all_to_all | solution.py:23
  17.0 584.9 %all-gather.6.cloned.1.call-start = ((), (), s32[]{:S(2)}) async-start(), calls=%async_computation.2 | async-start | bytes 2949120 | tf_op jit(solution)/shard_map/all_gather | solution.py:44
  222.4 5.0 collective-permute-start
  228.1 13.0 %collective-permute-start = (bf16[80,1024]{1,0:T(8,128)(2,1)}, bf16[80,1024]{1,0:T(8,128)(2,1)S(1)}, u32[]{:S(2)}, u32[]{:S(2)}) collective-permute-start(bf16[80,1024]{1,0:T(8,128)(2,1)} %get-tuple-element.420), channel_id=1, source_target_pairs={{0,64},{64,128},{128,192},{192,256},{256,320},{320,384},{384,448},... | collective-permute-start | bytes 491528 | tf_op jit(solution)/shard_map/while/body/eval_jaxpr/ppermute | solution.py:40
  241.8 6.8 %collective-permute-start = (bf16[80,1024]{1,0:T(8,128)(2,1)}, bf16[80,1024]{1,0:T(8,128)(2,1)S(1)}, u32[]{:S(2)}, u32[]{:S(2)}) collective-permute-start(bf16[80,1024]{1,0:T(8,128)(2,1)} %get-tuple-element.420), channel_id=1, source_target_pairs={{0,64},{64,128},{128,192},{192,256},{256,320},{320,384},{384,448},... | collective-permute-start | bytes 491528 | tf_op jit(solution)/shard_map/while/body/eval_jaxpr/ppermute | solution.py:40
  249.3 6.8 %collective-permute-start = (bf16[80,1024]{1,0:T(8,128)(2,1)}, bf16[80,1024]{1,0:T(8,128)(2,1)S(1)}, u32[]{:S(2)}, u32[]{:S(2)}) collective-permute-start(bf16[80,1024]{1,0:T(8,128)(2,1)} %get-tuple-element.420), channel_id=1, source_target_pairs={{0,64},{64,128},{128,192},{192,256},{256,320},{320,384},{384,448},... | collective-permute-start | bytes 491528 | tf_op jit(solution)/shard_map/while/body/eval_jaxpr/ppermute | solution.py:40
  256.8 6.8 %collective-permute-start = (bf16[80,1024]{1,0:T(8,128)(2,1)}, bf16[80,1024]{1,0:T(8,128)(2,1)S(1)}, u32[]{:S(2)}, u32[]{:S(2)}) collective-permute-start(bf16[80,1024]{1,0:T(8,128)(2,1)} %get-tuple-element.420), channel_id=1, source_target_pairs={{0,64},{64,128},{128,192},{192,256},{256,320},{320,384},{384,448},... | collective-permute-start | bytes 491528 | tf_op jit(solution)/shard_map/while/body/eval_jaxpr/ppermute | solution.py:40
  264.3 6.8 %collective-permute-start = (bf16[80,1024]{1,0:T(8,128)(2,1)}, bf16[80,1024]{1,0:T(8,128)(2,1)S(1)}, u32[]{:S(2)}, u32[]{:S(2)}) collective-permute-start(bf16[80,1024]{1,0:T(8,128)(2,1)} %get-tuple-element.420), channel_id=1, source_target_pairs={{0,64},{64,128},{128,192},{192,256},{256,320},{320,384},{384,448},... | collective-permute-start | bytes 491528 | tf_op jit(solution)/shard_map/while/body/eval_jaxpr/ppermute | solution.py:40
  271.9 92.8 %collective-permute-start = (bf16[80,1024]{1,0:T(8,128)(2,1)}, bf16[80,1024]{1,0:T(8,128)(2,1)S(1)}, u32[]{:S(2)}, u32[]{:S(2)}) collective-permute-start(bf16[80,1024]{1,0:T(8,128)(2,1)} %get-tuple-element.420), channel_id=1, source_target_pairs={{0,64},{64,128},{128,192},{192,256},{256,320},{320,384},{384,448},... | collective-permute-start | bytes 491528 | tf_op jit(solution)/shard_map/while/body/eval_jaxpr/ppermute | solution.py:40
  381.1 6.8 %collective-permute-start = (bf16[80,1024]{1,0:T(8,128)(2,1)}, bf16[80,1024]{1,0:T(8,128)(2,1)S(1)}, u32[]{:S(2)}, u32[]{:S(2)}) collective-permute-start(bf16[80,1024]{1,0:T(8,128)(2,1)} %get-tuple-element.420), channel_id=1, source_target_pairs={{0,64},{64,128},{128,192},{192,256},{256,320},{320,384},{384,448},... | collective-permute-start | bytes 491528 | tf_op jit(solution)/shard_map/while/body/eval_jaxpr/ppermute | solution.py:40
  404.3 6.8 %collective-permute-start = (bf16[80,1024]{1,0:T(8,128)(2,1)}, bf16[80,1024]{1,0:T(8,128)(2,1)S(1)}, u32[]{:S(2)}, u32[]{:S(2)}) collective-permute-start(bf16[80,1024]{1,0:T(8,128)(2,1)} %get-tuple-element.420), channel_id=1, source_target_pairs={{0,64},{64,128},{128,192},{192,256},{256,320},{320,384},{384,448},... | collective-permute-start | bytes 491528 | tf_op jit(solution)/shard_map/while/body/eval_jaxpr/ppermute | solution.py:40
  427.5 6.8 %collective-permute-start = (bf16[80,1024]{1,0:T(8,128)(2,1)}, bf16[80,1024]{1,0:T(8,128)(2,1)S(1)}, u32[]{:S(2)}, u32[]{:S(2)}) collective-permute-start(bf16[80,1024]{1,0:T(8,128)(2,1)} %get-tuple-element.420), channel_id=1, source_target_pairs={{0,64},{64,128},{128,192},{192,256},{256,320},{320,384},{384,448},... | collective-permute-start | bytes 491528 | tf_op jit(solution)/shard_map/while/body/eval_jaxpr/ppermute | solution.py:40
  450.7 6.8 %collective-permute-start = (bf16[80,1024]{1,0:T(8,128)(2,1)}, bf16[80,1024]{1,0:T(8,128)(2,1)S(1)}, u32[]{:S(2)}, u32[]{:S(2)}) collective-permute-start(bf16[80,1024]{1,0:T(8,128)(2,1)} %get-tuple-element.420), channel_id=1, source_target_pairs={{0,64},{64,128},{128,192},{192,256},{256,320},{320,384},{384,448},... | collective-permute-start | bytes 491528 | tf_op jit(solution)/shard_map/while/body/eval_jaxpr/ppermute | solution.py:40
  474.0 6.8 %collective-permute-start = (bf16[80,1024]{1,0:T(8,128)(2,1)}, bf16[80,1024]{1,0:T(8,128)(2,1)S(1)}, u32[]{:S(2)}, u32[]{:S(2)}) collective-permute-start(bf16[80,1024]{1,0:T(8,128)(2,1)} %get-tuple-element.420), channel_id=1, source_target_pairs={{0,64},{64,128},{128,192},{192,256},{256,320},{320,384},{384,448},... | collective-permute-start | bytes 491528 | tf_op jit(solution)/shard_map/while/body/eval_jaxpr/ppermute | solution.py:40
  497.2 6.8 %collective-permute-start = (bf16[80,1024]{1,0:T(8,128)(2,1)}, bf16[80,1024]{1,0:T(8,128)(2,1)S(1)}, u32[]{:S(2)}, u32[]{:S(2)}) collective-permute-start(bf16[80,1024]{1,0:T(8,128)(2,1)} %get-tuple-element.420), channel_id=1, source_target_pairs={{0,64},{64,128},{128,192},{192,256},{256,320},{320,384},{384,448},... | collective-permute-start | bytes 491528 | tf_op jit(solution)/shard_map/while/body/eval_jaxpr/ppermute | solution.py:40
  520.4 6.8 %collective-permute-start = (bf16[80,1024]{1,0:T(8,128)(2,1)}, bf16[80,1024]{1,0:T(8,128)(2,1)S(1)}, u32[]{:S(2)}, u32[]{:S(2)}) collective-permute-start(bf16[80,1024]{1,0:T(8,128)(2,1)} %get-tuple-element.420), channel_id=1, source_target_pairs={{0,64},{64,128},{128,192},{192,256},{256,320},{320,384},{384,448},... | collective-permute-start | bytes 491528 | tf_op jit(solution)/shard_map/while/body/eval_jaxpr/ppermute | solution.py:40
  543.6 3.9 collective-permute-start
Sparse Core Ops, SparseCore 0:
  11.8 197.7 all-gather.3
  552.0 49.8 all-gather.5
where the time goes:
time: 613 us; the launch traced here: 610 us
  waiting for transfers between devices  378 us (62%)
  matrix products  91.7 us (15%)
  local copies, waits for them, and re-layouts  68.9 us (11%)
  other arithmetic  31.1 us (5%)
  starting transfers between devices  25.9 us (4%)
  between operations  13.5 us (2%)
    all_gather x1, waiting for transfers between devices, gather_turned(): lax.all_gather(both, axis, axis=0, tiled=True)  166 us
    ppermute x15, waiting for transfers between devices, from_behind(): return lax.ppermute(block, axis, route)  138 us
    all_gather x1, waiting for transfers between devices, broadcast(): lax.all_gather(shard, axis)  50 us
    dot_general x8, matrix products, attend_layer(): jnp.dot(normed, qkv_weight, preferred_element_type=jnp.float32)  33.3 us
    all_to_all x1, waiting for transfers between devices, copy_for_each(): return lax.all_to_all(copies, axis, split_axis=0, concat_axis=0, tiled=True)  24.2 us
    reshape x24, local copies, waits for them, and re-layouts, split_heads(): return block.reshape(patch_count, PATCH, HEADS, head_dim)  20.8 us
    dot_general x8, matrix products, attend_layer(): jnp.einsum('phqk,pkhd->pqhd', weights, value_rows, preferred_element_type...  20.1 us
    ppermute x15, starting transfers between devices, from_behind(): return lax.ppermute(block, axis, route)  19.2 us
  transfers between devices with their start and end apart: 18, of which 17 were waited for; matrix products, arithmetic and copies ran while one was open for 6% of the time, Pallas kernels for 0%

commit v1 on v0

--- a/solution.py
+++ b/solution.py
@@ -10,7 +10,13 @@
 def gather_turned(arrays, axis, dims):
     turned = [jnp.moveaxis(a, dim, 0) for a, dim in zip(arrays, dims)]
     both = jnp.concatenate([t.reshape(len(t), -1) for t in turned], axis=1)
-    filled, at, gathered = (lax.all_gather(both, axis, axis=0, tiled=True), 0, [])
+    filled, at, gathered = (
+        jnp.concatenate(
+            lax.all_to_all(jnp.stack([both] * lax.axis_size(axis)), axis, 0, 0), axis=0
+        ),
+        0,
+        [],
+    )
     for t, dim in zip(turned, dims):
         piece = filled[:, at : at + t[0].size].reshape(-1, *t.shape[1:])
         gathered.append(jnp.moveaxis(piece, 0, dim))

time: 613 us -> 728 us (1.19)
  waiting for transfers between devices: 378 us -> 471 us
  starting transfers between devices: 25.9 us -> 44.5 us
    all_to_all x0 -> x1, waiting for transfers between devices: none -> 264 us  [gather_turned(): lax.all_to_all(jnp.stack([both] * lax.axis_size(axis)), axis, 0, 0)]
    all_gather x1 -> x0, waiting for transfers between devices: 166 us -> none  [gather_turned(): lax.all_gather(both, axis, axis=0, tiled=True)]
    all_to_all x0 -> x1, starting transfers between devices: none -> 18.6 us  [gather_turned(): lax.all_to_all(jnp.stack([both] * lax.axis_size(axis)), axis, 0, 0)]
    ppermute x15, waiting for transfers between devices: 138 us -> 123 us  [from_behind(): return lax.ppermute(block, axis, route)]
    all_gather x1, waiting for transfers between devices: 50 us -> 60.6 us  [broadcast(): lax.all_gather(shard, axis)]
  transfers between devices with their start and end apart: 18 -> 18, of which waited for: 17 -> 17; matrix products, arithmetic and copies ran while one was open for 6% -> 5% of each run, Pallas kernels for 0% -> 0%
where the time goes in v1:
time: 728 us; the launch traced here: 725 us
  waiting for transfers between devices  471 us (65%)
  matrix products  92.3 us (13%)
  local copies, waits for them, and re-layouts  73.3 us (10%)
  starting transfers between devices  44.5 us (6%)
  other arithmetic  29.5 us (4%)
  between operations  13.6 us (2%)
    all_to_all x1, waiting for transfers between devices, gather_turned(): lax.all_to_all(jnp.stack([both] * lax.axis_size(axis)), axis, 0, 0)  264 us
    ppermute x15, waiting for transfers between devices, from_behind(): return lax.ppermute(block, axis, route)  123 us
    all_gather x1, waiting for transfers between devices, broadcast(): lax.all_gather(shard, axis)  60.6 us
    dot_general x8, matrix products, attend_layer(): jnp.dot(normed, qkv_weight, preferred_element_type=jnp.float32)  33.3 us
    all_to_all x1, waiting for transfers between devices, copy_for_each(): return lax.all_to_all(copies, axis, split_axis=0, concat_axis=0, tiled=True)  23.9 us
    reshape x24, local copies, waits for them, and re-layouts, split_heads(): return block.reshape(patch_count, PATCH, HEADS, head_dim)  20.8 us
    dot_general x8, matrix products, attend_layer(): jnp.einsum('phqk,pkhd->pqhd', weights, value_rows, preferred_element_type...  20.6 us
    ppermute x15, starting transfers between devices, from_behind(): return lax.ppermute(block, axis, route)  19.2 us
  transfers between devices with their start and end apart: 18, of which 17 were waited for; matrix products, arithmetic and copies ran while one was open for 5% of the time, Pallas kernels for 0%

profile of v1, /device:TPU:57, one launch (start us, length us, event | category | flops | bytes accessed | tf_op | source)
XLA Modules:
  0.0 725.2 jit_solution(10508697882519969304)
XLA Ops:
  6.5 2.0 broadcast_in_dim.54
  8.6 6.7 all-to-all-start.1
  15.3 23.9 %all-to-all-done.1 = bf16[8,1,10,4096]{3,2,1,0:T(8,128)(2,1)S(1)} async-done(((bf16[8,1,10,4096]{3,2,1,0:T(8,128)(2,1)}), bf16[8,1,10,4096]{3,2,1,0:T(8,128)(2,1)S(1)}, u32[]{:S(2)}, u32[]{:S(2)}) %all-to-all-start.1) | async-done | bytes 655392 | tf_op jit(solution)/shard_map/all_to_all | solution.py:29
  39.2 4.4 stack.2
  43.6 18.6 %all-to-all-start = ((bf16[64,16,4864]{2,1,0:T(8,128)(2,1)}), bf16[64,16,4864]{2,1,0:T(8,128)(2,1)}, u32[]{:S(2)}, u32[]{:S(2)}) async-start(bf16[64,16,4864]{2,1,0:T(8,128)(2,1)} %stack.2), calls=%async_computation | async-start | bytes 19922944 | tf_op jit(solution)/shard_map/all_to_all | solution.py:15
  64.7 264.2 %all-to-all-done = bf16[64,16,4864]{2,1,0:T(8,128)(2,1)} async-done(((bf16[64,16,4864]{2,1,0:T(8,128)(2,1)}), bf16[64,16,4864]{2,1,0:T(8,128)(2,1)}, u32[]{:S(2)}, u32[]{:S(2)}) %all-to-all-start) | async-done | bytes 9961504 | tf_op jit(solution)/shard_map/all_to_all | solution.py:15
  328.9 5.9 slice.42
  334.8 1.8 slice.43
  336.5 3.2 convolution_convert_fusion.2
  341.0 310.8 %while.16 = (s32[]{:T(128)}, bf16[80,1024]{1,0:T(8,128)(2,1)S(1)}, bf16[8,80,1024]{2,1,0:T(8,128)(2,1)}, s32[]{:T(128)}, pred[]{:T(512)}, /*index=5*/bf16[8,80,1...) while((s32[]{:T(128)}, bf16[80,1024]{1,0:T(8,128)(2,1)S(1)}, ...), condition=%wide.region_6.7_spmd, body=%wide.region_0.6_spmd.sunk | while | flops 676917632 | bytes 15702796 | solution.py:154
  349.2 3.9 collective-permute-done
  356.8 3.9 collective-permute-done
  364.3 3.9 collective-permute-done
  371.8 3.9 collective-permute-done
  379.3 3.9 collective-permute-done
  386.8 81.5 %collective-permute-done = bf16[80,1024]{1,0:T(8,128)(2,1)S(1)} collective-permute-done((bf16[80,1024]{1,0:T(8,128)(2,1)}, bf16[80,1024]{1,0:T(8,128)(2,1)S(1)}, u32[]{:S(2)}, u32[]{:S(2)}) %collective-permute-start) | collective-permute-done | bytes 163872 | tf_op jit(solution)/shard_map/while/body/eval_jaxpr/ppermute | solution.py:46
  468.3 16.5 %conditional.2 = (bf16[80,1024]{1,0:T(8,128)(2,1)}) conditional(s32[]{:T(128)} %convert_element_type.127, () %tuple.47, (pred[]{:T(512)}, bf16[8,80,1024]{2,1,0:T(8,128)(2,1)}, s32[]{:T(128)}, bf16[80,1024]{1,0:T(8,128)(2,1)S(1)}, bf16[8,80,1024]{2,1,0:T(8,128)(2,1)}, /*index=5*/bf16[1024]{0:T(1024)(128)(2,1)S(1)}, bf16[1024,3072]{1,0:T(8,128)(2,1)}, ...), branch_computations={%region_1.1_spmd, %region_2.5_spmd} | conditional | flops 676835712 | bytes 14227409 | solution.py:137
  469.5 4.2 convolution_convert_fusion
  478.9 2.6 fusion.4
  482.7 2.1 fusion.5
  487.0 1.6 bitcast_dynamic-update-slice_fusion.2
  488.6 3.0 collective-permute-done
  491.6 16.5 %conditional.2 = (bf16[80,1024]{1,0:T(8,128)(2,1)}) conditional(s32[]{:T(128)} %convert_element_type.127, () %tuple.47, (pred[]{:T(512)}, bf16[8,80,1024]{2,1,0:T(8,128)(2,1)}, s32[]{:T(128)}, bf16[80,1024]{1,0:T(8,128)(2,1)S(1)}, bf16[8,80,1024]{2,1,0:T(8,128)(2,1)}, /*index=5*/bf16[1024]{0:T(1024)(128)(2,1)S(1)}, bf16[1024,3072]{1,0:T(8,128)(2,1)}, ...), branch_computations={%region_1.1_spmd, %region_2.5_spmd} | conditional | flops 676835712 | bytes 14227409 | solution.py:137
  492.8 4.2 convolution_convert_fusion
  502.2 2.6 fusion.4
  506.0 2.1 fusion.5
  510.3 1.6 bitcast_dynamic-update-slice_fusion.2
  511.9 3.0 collective-permute-done
  514.9 16.5 %conditional.2 = (bf16[80,1024]{1,0:T(8,128)(2,1)}) conditional(s32[]{:T(128)} %convert_element_type.127, () %tuple.47, (pred[]{:T(512)}, bf16[8,80,1024]{2,1,0:T(8,128)(2,1)}, s32[]{:T(128)}, bf16[80,1024]{1,0:T(8,128)(2,1)S(1)}, bf16[8,80,1024]{2,1,0:T(8,128)(2,1)}, /*index=5*/bf16[1024]{0:T(1024)(128)(2,1)S(1)}, bf16[1024,3072]{1,0:T(8,128)(2,1)}, ...), branch_computations={%region_1.1_spmd, %region_2.5_spmd} | conditional | flops 676835712 | bytes 14227409 | solution.py:137
  516.1 4.2 convolution_convert_fusion
  525.5 2.6 fusion.4
  529.3 2.1 fusion.5
  533.6 1.6 bitcast_dynamic-update-slice_fusion.2
  535.2 3.0 collective-permute-done
  538.2 16.5 %conditional.2 = (bf16[80,1024]{1,0:T(8,128)(2,1)}) conditional(s32[]{:T(128)} %convert_element_type.127, () %tuple.47, (pred[]{:T(512)}, bf16[8,80,1024]{2,1,0:T(8,128)(2,1)}, s32[]{:T(128)}, bf16[80,1024]{1,0:T(8,128)(2,1)S(1)}, bf16[8,80,1024]{2,1,0:T(8,128)(2,1)}, /*index=5*/bf16[1024]{0:T(1024)(128)(2,1)S(1)}, bf16[1024,3072]{1,0:T(8,128)(2,1)}, ...), branch_computations={%region_1.1_spmd, %region_2.5_spmd} | conditional | flops 676835712 | bytes 14227409 | solution.py:137
  539.4 4.2 convolution_convert_fusion
  548.8 2.6 fusion.4
  552.6 2.1 fusion.5
  556.9 1.7 bitcast_dynamic-update-slice_fusion.2
  558.6 2.9 collective-permute-done
  561.5 16.5 %conditional.2 = (bf16[80,1024]{1,0:T(8,128)(2,1)}) conditional(s32[]{:T(128)} %convert_element_type.127, () %tuple.47, (pred[]{:T(512)}, bf16[8,80,1024]{2,1,0:T(8,128)(2,1)}, s32[]{:T(128)}, bf16[80,1024]{1,0:T(8,128)(2,1)S(1)}, bf16[8,80,1024]{2,1,0:T(8,128)(2,1)}, /*index=5*/bf16[1024]{0:T(1024)(128)(2,1)S(1)}, bf16[1024,3072]{1,0:T(8,128)(2,1)}, ...), branch_computations={%region_1.1_spmd, %region_2.5_spmd} | conditional | flops 676835712 | bytes 14227409 | solution.py:137
  562.7 4.2 convolution_convert_fusion
  572.1 2.6 fusion.4
  575.9 2.1 fusion.5
  581.8 3.0 collective-permute-done
  584.8 16.5 %conditional.2 = (bf16[80,1024]{1,0:T(8,128)(2,1)}) conditional(s32[]{:T(128)} %convert_element_type.127, () %tuple.47, (pred[]{:T(512)}, bf16[8,80,1024]{2,1,0:T(8,128)(2,1)}, s32[]{:T(128)}, bf16[80,1024]{1,0:T(8,128)(2,1)S(1)}, bf16[8,80,1024]{2,1,0:T(8,128)(2,1)}, /*index=5*/bf16[1024]{0:T(1024)(128)(2,1)S(1)}, bf16[1024,3072]{1,0:T(8,128)(2,1)}, ...), branch_computations={%region_1.1_spmd, %region_2.5_spmd} | conditional | flops 676835712 | bytes 14227409 | solution.py:137
  586.0 4.2 convolution_convert_fusion
  595.4 2.6 fusion.4
  599.2 2.1 fusion.5
  603.5 1.6 bitcast_dynamic-update-slice_fusion.2
  605.1 3.0 collective-permute-done
  608.1 16.5 %conditional.2 = (bf16[80,1024]{1,0:T(8,128)(2,1)}) conditional(s32[]{:T(128)} %convert_element_type.127, () %tuple.47, (pred[]{:T(512)}, bf16[8,80,1024]{2,1,0:T(8,128)(2,1)}, s32[]{:T(128)}, bf16[80,1024]{1,0:T(8,128)(2,1)S(1)}, bf16[8,80,1024]{2,1,0:T(8,128)(2,1)}, /*index=5*/bf16[1024]{0:T(1024)(128)(2,1)S(1)}, bf16[1024,3072]{1,0:T(8,128)(2,1)}, ...), branch_computations={%region_1.1_spmd, %region_2.5_spmd} | conditional | flops 676835712 | bytes 14227409 | solution.py:137
  609.3 4.2 convolution_convert_fusion
  618.7 2.6 fusion.4
  622.5 2.1 fusion.5
  626.8 1.6 bitcast_dynamic-update-slice_fusion.2
  628.4 3.0 collective-permute-done
  631.4 16.5 %conditional.2 = (bf16[80,1024]{1,0:T(8,128)(2,1)}) conditional(s32[]{:T(128)} %convert_element_type.127, () %tuple.47, (pred[]{:T(512)}, bf16[8,80,1024]{2,1,0:T(8,128)(2,1)}, s32[]{:T(128)}, bf16[80,1024]{1,0:T(8,128)(2,1)S(1)}, bf16[8,80,1024]{2,1,0:T(8,128)(2,1)}, /*index=5*/bf16[1024]{0:T(1024)(128)(2,1)S(1)}, bf16[1024,3072]{1,0:T(8,128)(2,1)}, ...), branch_computations={%region_1.1_spmd, %region_2.5_spmd} | conditional | flops 676835712 | bytes 14227409 | solution.py:137
  632.6 4.2 convolution_convert_fusion
  642.0 2.6 fusion.4
  645.8 2.1 fusion.5
  651.7 1.7 fusion.19
  653.4 2.7 fusion.29
  656.2 60.6 %all-gather.3.cloned.1.call-done = bf16[64,80,256]{2,1,0:T(8,128)(2,1)} async-done(((bf16[8,80,256]{2,1,0:T(8,128)(2,1)}), bf16[64,80,256]{2,1,0:T(8,128)(2,1)}) %all-gather.3.cloned.1.call-update) | async-done | bytes 2621456 | tf_op jit(solution)/shard_map/all_gather | solution.py:50
  (186 shorter events, 118.1 us)
Async XLA Ops:
  6.5 56.1 %copy-start = (bf16[256,1024]{1,0:T(8,128)(2,1)S(1)}, bf16[256,1024]{1,0:T(8,128)(2,1)}, u32[]{:S(2)}) copy-start(bf16[256,1024]{1,0:T(8,128)(2,1)} %param.17) | copy-start | bytes 1572868
  6.5 8.7 %copy-start.1 = (bf16[1,16,3072]{2,1,0:T(8,128)(2,1)S(1)}, bf16[1,16,3072]{2,1,0:T(8,128)(2,1)}, u32[]{:S(2)}) copy-start(bf16[1,16,3072]{2,1,0:T(8,128)(2,1)} %param.18) | copy-start | bytes 294916
  6.5 8.7 %copy-start.2 = (bf16[1,16,1024]{2,1,0:T(8,128)(2,1)S(1)}, bf16[1,16,1024]{2,1,0:T(8,128)(2,1)}, u32[]{:S(2)}) copy-start(bf16[1,16,1024]{2,1,0:T(8,128)(2,1)} %param.19) | copy-start | bytes 98308
  6.5 8.7 %copy-start.3 = (bf16[512,16]{0,1:T(8,128)(2,1)S(1)}, bf16[512,16]{0,1:T(8,128)(2,1)}, u32[]{:S(2)}) copy-start(bf16[512,16]{0,1:T(8,128)(2,1)} %param.21) | copy-start | bytes 49156
  6.5 8.8 %copy-start.4 = (bf16[256,16]{0,1:T(8,128)(2,1)S(1)}, bf16[256,16]{0,1:T(8,128)(2,1)}, u32[]{:S(2)}) copy-start(bf16[256,16]{0,1:T(8,128)(2,1)} %param.23) | copy-start | bytes 24580
  8.6 30.6 %all-to-all-start.1 = ((bf16[8,1,10,4096]{3,2,1,0:T(8,128)(2,1)}), bf16[8,1,10,4096]{3,2,1,0:T(8,128)(2,1)S(1)}, u32[]{:S(2)}, u32[]{:S(2)}) async-start(bf16[8,1,10,4096]{3,2,1,0:T(8,128)(2,1)} %broadcast_in_dim.54), calls=%async_computation.1 | async-start | bytes 2097152 | tf_op jit(solution)/shard_map/all_to_all | solution.py:29
  43.6 18.6 %copy-start.6 = (s32[8,80]{1,0:T(8,128)S(1)}, s32[8,80]{1,0:T(8,128)}, u32[]{:S(2)}) copy-start(s32[8,80]{1,0:T(8,128)} %param.14) | copy-start | bytes 7684
  43.6 18.9 %copy-start.7 = (bf16[1024]{0:T(1024)(128)(2,1)S(1)}, bf16[1024]{0:T(1024)(128)(2,1)}, u32[]{:S(2)}) copy-start(bf16[1024]{0:T(1024)(128)(2,1)} %param.22) | copy-start | bytes 6148
  43.6 18.9 %copy-start.5 = (bf16[1,1024]{1,0:T(2,128)(2,1)S(1)}, bf16[1,1024]{1,0:T(2,128)(2,1)}, u32[]{:S(2)}) copy-start(bf16[1,1024]{1,0:T(2,128)(2,1)} %param.20) | copy-start | bytes 6148
  43.6 19.0 %copy-start.8 = (s32[8]{0:T(128)S(1)}, s32[8]{0:T(128)}, u32[]{:S(2)}) copy-start(s32[8]{0:T(128)} %param.15) | copy-start | bytes 100
  43.6 285.3 %all-to-all-start = ((bf16[64,16,4864]{2,1,0:T(8,128)(2,1)}), bf16[64,16,4864]{2,1,0:T(8,128)(2,1)}, u32[]{:S(2)}, u32[]{:S(2)}) async-start(bf16[64,16,4864]{2,1,0:T(8,128)(2,1)} %stack.2), calls=%async_computation | async-start | bytes 19922944 | tf_op jit(solution)/shard_map/all_to_all | solution.py:15
  62.2 654.6 %all-gather.3.cloned.1.call-start = ((), (), s32[]{:S(2)}) async-start(), calls=%async_computation.2 | async-start | bytes 2949120 | tf_op jit(solution)/shard_map/all_gather | solution.py:50
  341.7 3.9 collective-permute-start
  346.3 6.8 collective-permute-start
  353.8 6.8 collective-permute-start
  361.3 6.8 collective-permute-start
  368.8 6.8 collective-permute-start
  376.4 6.8 collective-permute-start
  383.9 84.4 %collective-permute-start = (bf16[80,1024]{1,0:T(8,128)(2,1)}, bf16[80,1024]{1,0:T(8,128)(2,1)S(1)}, u32[]{:S(2)}, u32[]{:S(2)}) collective-permute-start(bf16[80,1024]{1,0:T(8,128)(2,1)} %get-tuple-element.420), channel_id=1, source_target_pairs={{0,64},{64,128},{128,192},{192,256},{256,320},{320,384},{384,448},... | collective-permute-start | bytes 491528 | tf_op jit(solution)/shard_map/while/body/eval_jaxpr/ppermute | solution.py:46
  484.8 6.8 collective-permute-start
  508.1 6.8 collective-permute-start
  531.4 6.8 collective-permute-start
  554.7 6.8 collective-permute-start
  578.0 6.8 collective-permute-start
  601.3 6.8 collective-permute-start
  624.6 6.8 collective-permute-start
  647.9 3.9 collective-permute-start
Sparse Core Ops, SparseCore 0:
  656.3 60.4 all-gather.2
